TPU v7x, 32 devices: a whole 2x2x4 slice. The times are simulated.
32 devices in a mesh: path: 8 (over z, core), tm: 4 (over y, x).
Axes of the slice: x: 2, y: 2, z: 4, core: 2. Of those that a mesh axis runs over, the one named last changes fastest.
Arguments:
- shock_rate: float32 [64, 131072], P('tm', 'path'), may hold values from -6 to 6
- shock_fx: float32 [4, 64, 131072], P(None, 'tm', 'path'), may hold values from -6 to 6
- fx_vol: float32 [4], replicated, may hold values from 0.1 to 0.4
- fx_corr: float32 [4], replicated, may hold values from -0.8 to 0.8
- hazard_scale: float32 [32], replicated, may hold values from 0.03 to 3
- counterparty: int32 [512], replicated, may hold values from 0 to 31
- currency: int32 [512], replicated, may hold values from 0 to 3
- maturity: int32 [512], replicated, may hold values from 1 to 64
- notional: float32 [512], replicated, may hold values from -8 to 8
- strike: float32 [512], replicated, may hold values from 0.7 to 1.3
Outputs:
- profile: float32 [64, 32], P('tm')
- cva: float32 [32], replicated
All inputs are finite; a program needn't handle non-finite values.
Results may differ from a plain program's by a relative error of at most 0.000061.
Values sent between devices are 32-bit elements; how exact they have to be, the bound alone decides.
A program may use at most 64 MiB of HBM per device.

v0:
```python
import math
import jax
import jax.numpy as jnp
from jax import lax
from jax.sharding import PartitionSpec as P

HORIZON = 5.0
RATE_DOM = 0.03
RATE_FOR = 0.01
LOSS_SHARE = 0.6
RATE_SHIFT = 1.5
HIGHEST_PREC = lax.Precision.HIGHEST


def carried_in(part, axis, combine, identity):
    place = lax.axis_index(axis)
    gathered = jax.tree.map(lambda a: lax.all_gather(a, axis), part)
    state = jax.tree.map(lambda a, e: jnp.zeros_like(a) + jnp.asarray(e, a.dtype), part, identity)

    def one(turn, state):
        return combine(
            state, jax.tree.map(lambda a: lax.dynamic_index_in_dim(a, turn, 0, False), gathered)
        )

    return lax.fori_loop(0, place, one, state)


def trade_tables(
    date_rows, counterparty, currency, maturity, notional, strike, cp_count, ccy_count, date_step
):
    is_alive = (date_rows[:, None] < maturity[None, :]).astype(jnp.float32)
    time_left = (maturity[None, :] - date_rows[:, None]).astype(jnp.float32) * date_step
    weight_for = is_alive * notional[None, :] * jnp.exp(-RATE_FOR * time_left)
    weight_dom = is_alive * (notional * strike)[None, :] * jnp.exp(-RATE_DOM * time_left)
    member = (counterparty[None, :] == jnp.arange(cp_count, dtype=jnp.int32)[:, None]).astype(
        jnp.float32
    )
    currency_onehot = (currency[None, :] == jnp.arange(ccy_count, dtype=jnp.int32)[:, None]).astype(
        jnp.float32
    )
    fwd_table = jnp.einsum(
        "ck,tk,jk->tcj", member, weight_for, currency_onehot, precision=HIGHEST_PREC
    )
    dom_table = jnp.einsum("ck,tk->tc", member, weight_dom, precision=HIGHEST_PREC)
    return (fwd_table, dom_table)


def weigh_block(block_item, hazard_scale):
    fwd_table, dom_table, spot, hazard_prev, hazard_cur = block_item
    netted = (
        jnp.einsum("tcj,tjp->tcp", fwd_table, spot, precision=HIGHEST_PREC) - dom_table[:, :, None]
    )
    exposure = jnp.maximum(netted, 0.0)
    scale_row = hazard_scale[None, :, None]
    density = jnp.exp(-scale_row * hazard_prev[:, None, :]) - jnp.exp(
        -scale_row * hazard_cur[:, None, :]
    )
    return jnp.sum(exposure * density, axis=2)


def weigh_dates(fwd_table, dom_table, spot, hazard_prev, hazard_cur, hazard_scale):
    date_count, path_count = hazard_cur.shape
    cp_count = dom_table.shape[1]
    ccy_count = spot.shape[1]
    block_dates = math.gcd(date_count, max(1, 32768 // path_count))
    groups = date_count // block_dates
    blocks = (
        fwd_table.reshape(groups, block_dates, cp_count, ccy_count),
        dom_table.reshape(groups, block_dates, cp_count),
        spot.reshape(groups, block_dates, ccy_count, path_count),
        hazard_prev.reshape(groups, block_dates, path_count),
        hazard_cur.reshape(groups, block_dates, path_count),
    )
    weighed = lax.map(lambda block_item: weigh_block(block_item, hazard_scale), blocks)
    return weighed.reshape(date_count, cp_count)


def local_walk(rate_shock, other_shock, fx_vol, fx_corr, date_step, decay_rate, noise_scale):
    date_count = rate_shock.shape[0]
    date_index = jnp.arange(date_count, dtype=jnp.int32)
    date_gap = date_index[:, None] - date_index[None, :]
    is_below = date_gap >= 0
    powers = jnp.where(is_below, decay_rate ** jnp.maximum(date_gap, 0).astype(jnp.float32), 0.0)
    lower_ones = is_below.astype(jnp.float32)
    rate_walk = noise_scale * jnp.dot(powers, rate_shock, precision=HIGHEST_PREC)
    mix_weight = jnp.sqrt(1.0 - fx_corr * fx_corr)
    mixed = fx_corr[:, None, None] * rate_shock[None] + mix_weight[:, None, None] * other_shock
    moves = (fx_vol * math.sqrt(date_step))[:, None, None] * mixed - (
        0.5 * fx_vol * fx_vol * date_step
    )[:, None, None]
    fx_walk = jnp.einsum("ts,jsp->tjp", lower_ones, moves, precision=HIGHEST_PREC)
    carry_gain = decay_rate ** (jnp.arange(date_count, dtype=jnp.float32) + 1.0)
    return (rate_walk, fx_walk, carry_gain, lower_ones)


def path_intensity(rate_walk, carry_gain, rate_in):
    shifted = rate_walk + carry_gain[:, None] * rate_in[None, :] + RATE_SHIFT
    return 0.1 + 0.5 * shifted * shifted


def finish_paths(intensity, lower_ones, fx_walk, hazard_in, log_in, date_step):
    hazard_cur = hazard_in[None, :] + date_step * jnp.dot(
        lower_ones, intensity, precision=HIGHEST_PREC
    )
    hazard_prev = hazard_cur - date_step * intensity
    spot = jnp.exp(fx_walk + log_in[None])
    return (hazard_prev, hazard_cur, spot)


def combine_affine(earlier, later):
    gain_a, end_a, log_a = earlier
    gain_b, end_b, log_b = later
    return (gain_b * gain_a, gain_b * end_a + end_b, log_a + log_b)


def combine_total(earlier, later):
    return earlier + later


def per_device(
    shock_rate,
    shock_fx,
    fx_vol,
    fx_corr,
    hazard_scale,
    counterparty,
    currency,
    maturity,
    notional,
    strike,
):
    local_dates = shock_rate.shape[0]
    total_dates = local_dates * lax.axis_size("tm")
    total_paths = shock_rate.shape[1] * lax.axis_size("path")
    cp_count = hazard_scale.shape[0]
    ccy_count = fx_vol.shape[0]
    date_step = HORIZON / total_dates
    decay_rate = math.exp(-2.0 / total_dates)
    noise_scale = math.sqrt(1.0 - decay_rate * decay_rate)
    first_date = lax.axis_index("tm") * local_dates
    rate_walk, fx_walk, carry_gain, lower_ones = local_walk(
        shock_rate, shock_fx, fx_vol, fx_corr, date_step, decay_rate, noise_scale
    )
    blank = jnp.zeros_like(rate_walk[0])
    span_gain = jnp.full((1,), decay_rate**local_dates, jnp.float32)
    unit_gain = jnp.ones((1,), jnp.float32)
    log_blank = jnp.zeros_like(fx_walk[0])
    carried = carried_in(
        (span_gain, rate_walk[-1], fx_walk[-1]), "tm", combine_affine, (unit_gain, blank, log_blank)
    )
    rate_in, log_in = (carried[1], carried[2])
    intensity = path_intensity(rate_walk, carry_gain, rate_in)
    block_total = date_step * jnp.sum(intensity, axis=0)
    hazard_in = carried_in(block_total, "tm", combine_total, blank)
    hazard_prev, hazard_cur, spot = finish_paths(
        intensity, lower_ones, fx_walk, hazard_in, log_in, date_step
    )
    date_rows = first_date + jnp.arange(local_dates, dtype=jnp.int32)
    fwd_table, dom_table = trade_tables(
        date_rows,
        counterparty,
        currency,
        maturity,
        notional,
        strike,
        cp_count,
        ccy_count,
        date_step,
    )
    local_sum = weigh_dates(fwd_table, dom_table, spot, hazard_prev, hazard_cur, hazard_scale)
    discount = jnp.exp(-RATE_DOM * date_step * (jnp.arange(total_dates, dtype=jnp.float32) + 1.0))
    profile = lax.psum(local_sum, "path") / (total_paths * date_step)
    own_discount = lax.dynamic_slice_in_dim(discount, first_date, local_dates, 0)
    cva = lax.psum(LOSS_SHARE * date_step * jnp.sum(own_discount[:, None] * profile, axis=0), "tm")
    return (profile, cva)


def solution(mesh):
    return jax.shard_map(
        per_device,
        mesh=mesh,
        in_specs=(P("tm", "path"), P(None, "tm", "path"), P(), P(), P(), P(), P(), P(), P(), P()),
        out_specs=(P("tm", None), P()),
        check_vma=False,
    )
```

profile of v0, /device:TPU:0, one launch (start us, length us, event | category | flops | bytes accessed | tf_op | source)
XLA Modules:
  0.0 156.9 jit_solution(9286434855395764987)
XLA Ops:
  7.9 5.5 %fusion.8 = f32[16,4,16384]{2,0,1:T(8,128)S(1)} fusion(f32[4,16,16384]{2,1,0:T(8,128)} %param.17, f32[4]{0:T(128)S(1)} %get-tuple-element.248, f32[4]{0:T(128)S(1)} %get-tuple-element.251, f32[16,16384]{1,0:T(8,128)} %param.16, f32[4]{0:T(128)} %param.19, f32[4]{0:T(128)S(1)} %get-tuple-element.247), kind=kOutput, calls=%fused_computation.23 | convolution fusion | flops 206569984 | bytes 9437248 | tf_op jit(solution)/shard_map/ts,jsp->tjp/dot_general | solution.py:91
  13.4 1.9 %copy-done = f32[16,4,16384]{2,0,1:T(8,128)} copy-done((f32[16,4,16384]{2,0,1:T(8,128)}, f32[16,4,16384]{2,0,1:T(8,128)S(1)}, u32[]{:S(2)}) %copy-start) | copy-done | bytes 4194328
  15.6 0.9 copy.15
  16.6 1.0 convolution_multiply_fusion.1
  17.6 10.5 %all-gather.1 = f32[4,1,16384]{2,1,0:T(1,128)S(1)} all-gather(f32[1,1,16384]{2,1,0:T(1,128)S(1)} %slice_bitcast_fusion), channel_id=1, replica_groups=mesh['path'=8,'tm'=4] {'tm'}, dimensions={0}, use_global_device_ids=true | all-gather | bytes 327680 | tf_op jit(solution)/shard_map/all_gather | solution.py:17
  28.7 0.8 dynamic-update-slice
  29.5 8.9 %all-reduce = f32[4]{0:T(128)S(1)} all-reduce(f32[4]{0:T(128)S(1)} %dynamic-update-slice), channel_id=1, replica_groups=mesh['path'=8,'tm'=4] {'tm'}, use_global_device_ids=true, to_apply=%add | all-reduce | flops 4 | bytes 32
  39.3 6.6 %all-gather.4.cloned.1.call-done = f32[4,4,16384]{2,1,0:T(4,128)} async-done(((f32[1,4,16384]{2,1,0:T(4,128)}), f32[4,4,16384]{2,1,0:T(4,128)}) %all-gather.4.cloned.1.call-update) | async-done | bytes 1048592 | tf_op jit(solution)/shard_map/all_gather | solution.py:17
  46.0 2.7 %add_exponential_fusion = f32[16,4,16384]{2,0,1:T(8,128)S(1)} fusion(f32[16,4,16384]{2,0,1:T(8,128)} %copy-done, f32[4,16384]{1,0:T(4,128)S(1)} %get-tuple-element.178), kind=kLoop, calls=%fused_computation.22 | loop fusion | flops 1048576 | bytes 8650752 | tf_op jit(solution)/shard_map/exp | solution.py:106
  48.7 4.6 %copy.18 = f32[16,4,16384]{2,1,0:T(4,128)} copy(f32[16,4,16384]{2,0,1:T(8,128)S(1)} %add_exponential_fusion) | data formatting | bytes 8388608 | tf_op jit(solution)/shard_map/while | solution.py:74
  53.8 15.0 %all-gather = f32[65536]{0:T(1024)S(1)} all-gather(f32[16384]{0:T(1024)S(1)} %broadcast_multiply_fusion), channel_id=2, replica_groups=mesh['path'=8,'tm'=4] {'tm'}, dimensions={0}, use_global_device_ids=true | all-gather | bytes 327680 | tf_op jit(solution)/shard_map/all_gather | solution.py:17
  69.1 2.1 %multiply_subtract_fusion = (f32[16,16384]{1,0:T(8,128)}, f32[16,16384]{1,0:T(8,128)S(1)}) fusion(f32[16,16384]{1,0:T(8,128)S(1)} %convolution_multiply_fusion.1, f32[16384]{0:T(1024)S(1)} %get-tuple-element.179, f32[16]{0:T(128)S(1)} %add_power_fusion, f32[16384]{0:T(1024)S(1)} %get-tuple-element.180), kind=kOutput, calls=%fused_computation.36 | convolution fusion | flops 54526464 | bytes 3276864 | tf_op jit(solution)/shard_map/dot_general | solution.py:102
  71.2 1.8 %reshape.69 = f32[8,2,16384]{2,1,0:T(2,128)S(1)} reshape(f32[16,16384]{1,0:T(8,128)} %get-tuple-element.249) | data formatting | bytes 2097152 | tf_op jit(solution)/shard_map/reshape | solution.py:71
  73.7 51.0 %while.38 = (s32[]{:T(128)}, f32[8,2,32]{2,1,0:T(2,128)S(1)}, f32[8,2,32,4]{2,1,0,3:T(2,128)S(1)}, f32[8,2,4,16384]{3,2,1,0:T(4,128)}, f32[8,2,32]{2,1,0:T(2,128...) while((s32[]{:T(128)}, f32[8,2,32]{2,1,0:T(2,128)S(1)}, ...), condition=%wide.region_7.8_spmd, body=%wide.region_5.7_spmd.sunk | while | flops 57671616 | bytes 1317113 | solution.py:74
  73.8 6.3 %fusion.73 = f32[2,32]{1,0:T(2,128)S(1)} fusion(f32[2,16384]{1,0:T(2,128)S(1)} %get-tuple-element.373, f32[2,16384]{1,0:T(2,128)S(1)} %get-tuple-element.374, f32[32]{0:T(128)S(1)} %bitcast.77, f32[2,32]{1,0:T(2,128)S(1)} %fusion.72, f32[8,2,4,16384]{3,2,1,0:T(4,128)} %get-tuple-element.447, s32[]{:T(128)S(6)} %copy.46, ...), kind=kOutput, calls=%fused_computation.8.clone.1 | convolution fusion | flops 57671616 | bytes 788100 | tf_op jit(solution)/shard_map/while/body/eval_jaxpr/tcj,tjp->tcp/dot_general | solution.py:51
  80.1 6.3 %fusion.73 = f32[2,32]{1,0:T(2,128)S(1)} fusion(f32[2,16384]{1,0:T(2,128)S(1)} %get-tuple-element.373, f32[2,16384]{1,0:T(2,128)S(1)} %get-tuple-element.374, f32[32]{0:T(128)S(1)} %bitcast.77, f32[2,32]{1,0:T(2,128)S(1)} %fusion.72, f32[8,2,4,16384]{3,2,1,0:T(4,128)} %get-tuple-element.447, s32[]{:T(128)S(6)} %copy.46, ...), kind=kOutput, calls=%fused_computation.8.clone.1 | convolution fusion | flops 57671616 | bytes 788100 | tf_op jit(solution)/shard_map/while/body/eval_jaxpr/tcj,tjp->tcp/dot_general | solution.py:51
  86.5 6.3 %fusion.73 = f32[2,32]{1,0:T(2,128)S(1)} fusion(f32[2,16384]{1,0:T(2,128)S(1)} %get-tuple-element.373, f32[2,16384]{1,0:T(2,128)S(1)} %get-tuple-element.374, f32[32]{0:T(128)S(1)} %bitcast.77, f32[2,32]{1,0:T(2,128)S(1)} %fusion.72, f32[8,2,4,16384]{3,2,1,0:T(4,128)} %get-tuple-element.447, s32[]{:T(128)S(6)} %copy.46, ...), kind=kOutput, calls=%fused_computation.8.clone.1 | convolution fusion | flops 57671616 | bytes 788100 | tf_op jit(solution)/shard_map/while/body/eval_jaxpr/tcj,tjp->tcp/dot_general | solution.py:51
  92.9 6.3 %fusion.73 = f32[2,32]{1,0:T(2,128)S(1)} fusion(f32[2,16384]{1,0:T(2,128)S(1)} %get-tuple-element.373, f32[2,16384]{1,0:T(2,128)S(1)} %get-tuple-element.374, f32[32]{0:T(128)S(1)} %bitcast.77, f32[2,32]{1,0:T(2,128)S(1)} %fusion.72, f32[8,2,4,16384]{3,2,1,0:T(4,128)} %get-tuple-element.447, s32[]{:T(128)S(6)} %copy.46, ...), kind=kOutput, calls=%fused_computation.8.clone.1 | convolution fusion | flops 57671616 | bytes 788100 | tf_op jit(solution)/shard_map/while/body/eval_jaxpr/tcj,tjp->tcp/dot_general | solution.py:51
  99.2 6.3 %fusion.73 = f32[2,32]{1,0:T(2,128)S(1)} fusion(f32[2,16384]{1,0:T(2,128)S(1)} %get-tuple-element.373, f32[2,16384]{1,0:T(2,128)S(1)} %get-tuple-element.374, f32[32]{0:T(128)S(1)} %bitcast.77, f32[2,32]{1,0:T(2,128)S(1)} %fusion.72, f32[8,2,4,16384]{3,2,1,0:T(4,128)} %get-tuple-element.447, s32[]{:T(128)S(6)} %copy.46, ...), kind=kOutput, calls=%fused_computation.8.clone.1 | convolution fusion | flops 57671616 | bytes 788100 | tf_op jit(solution)/shard_map/while/body/eval_jaxpr/tcj,tjp->tcp/dot_general | solution.py:51
  105.6 6.3 %fusion.73 = f32[2,32]{1,0:T(2,128)S(1)} fusion(f32[2,16384]{1,0:T(2,128)S(1)} %get-tuple-element.373, f32[2,16384]{1,0:T(2,128)S(1)} %get-tuple-element.374, f32[32]{0:T(128)S(1)} %bitcast.77, f32[2,32]{1,0:T(2,128)S(1)} %fusion.72, f32[8,2,4,16384]{3,2,1,0:T(4,128)} %get-tuple-element.447, s32[]{:T(128)S(6)} %copy.46, ...), kind=kOutput, calls=%fused_computation.8.clone.1 | convolution fusion | flops 57671616 | bytes 788100 | tf_op jit(solution)/shard_map/while/body/eval_jaxpr/tcj,tjp->tcp/dot_general | solution.py:51
  112.0 6.3 %fusion.73 = f32[2,32]{1,0:T(2,128)S(1)} fusion(f32[2,16384]{1,0:T(2,128)S(1)} %get-tuple-element.373, f32[2,16384]{1,0:T(2,128)S(1)} %get-tuple-element.374, f32[32]{0:T(128)S(1)} %bitcast.77, f32[2,32]{1,0:T(2,128)S(1)} %fusion.72, f32[8,2,4,16384]{3,2,1,0:T(4,128)} %get-tuple-element.447, s32[]{:T(128)S(6)} %copy.46, ...), kind=kOutput, calls=%fused_computation.8.clone.1 | convolution fusion | flops 57671616 | bytes 788100 | tf_op jit(solution)/shard_map/while/body/eval_jaxpr/tcj,tjp->tcp/dot_general | solution.py:51
  118.3 6.3 %fusion.73 = f32[2,32]{1,0:T(2,128)S(1)} fusion(f32[2,16384]{1,0:T(2,128)S(1)} %get-tuple-element.373, f32[2,16384]{1,0:T(2,128)S(1)} %get-tuple-element.374, f32[32]{0:T(128)S(1)} %bitcast.77, f32[2,32]{1,0:T(2,128)S(1)} %fusion.72, f32[8,2,4,16384]{3,2,1,0:T(4,128)} %get-tuple-element.447, s32[]{:T(128)S(6)} %copy.46, ...), kind=kOutput, calls=%fused_computation.8.clone.1 | convolution fusion | flops 57671616 | bytes 788100 | tf_op jit(solution)/shard_map/while/body/eval_jaxpr/tcj,tjp->tcp/dot_general | solution.py:51
  124.7 15.0 %psum.14 = f32[16,32]{1,0:T(8,128)S(1)} all-reduce(f32[16,32]{1,0:T(8,128)S(1)} %bitcast.74), channel_id=1, replica_groups=mesh['path'=8,'tm'=4] {'path'}, use_global_device_ids=true, to_apply=%region_8.9 | all-reduce | flops 512 | bytes 4096 | tf_op jit(solution)/shard_map/psum | solution.py:172
  140.3 9.7 %psum.15 = f32[32]{0:T(128)} all-reduce(f32[32]{0:T(128)S(1)} %broadcast_multiply_fusion.2), channel_id=1, replica_groups=mesh['path'=8,'tm'=4] {'tm'}, use_global_device_ids=true, to_apply=%region_10.11 | all-reduce | flops 32 | bytes 256 | tf_op jit(solution)/shard_map/psum | solution.py:174
  (79 shorter events, 4.9 us)
Async XLA Ops:
  7.2 38.8 %all-gather.4.cloned.1.call-start = ((), (), s32[]{:S(2)}) async-start(), calls=%async_computation | async-start | bytes 1310720 | tf_op jit(solution)/shard_map/all_gather | solution.py:17
  7.9 8.7 %copy-start.1 = (f32[16,16384]{1,0:T(8,128)S(1)}, f32[16,16384]{1,0:T(8,128)}, u32[]{:S(2)}) copy-start(f32[16,16384]{1,0:T(8,128)} %param.16) | copy-start | bytes 3145732
  7.9 20.2 %copy-start.8 = (u32[32]{0:T(128)S(1)}, u32[32]{0:T(128)}, u32[]{:S(2)}) copy-start(u32[32]{0:T(128)} %constant.112) | copy-start | bytes 388
  13.4 1.9 %copy-start = (f32[16,4,16384]{2,0,1:T(8,128)}, f32[16,4,16384]{2,0,1:T(8,128)S(1)}, u32[]{:S(2)}) copy-start(f32[16,4,16384]{2,0,1:T(8,128)S(1)} %fusion.8) | copy-start | bytes 12582916
  15.4 23.2 %copy-start.2 = (f32[512]{0:T(512)S(1)}, f32[512]{0:T(512)}, u32[]{:S(2)}) copy-start(f32[512]{0:T(512)} %param.24) | copy-start | bytes 6148
  15.4 23.2 %copy-start.3 = (f32[512]{0:T(512)S(1)}, f32[512]{0:T(512)}, u32[]{:S(2)}) copy-start(f32[512]{0:T(512)} %param.25) | copy-start | bytes 6148
  15.4 23.4 %copy-start.7 = (f32[32]{0:T(128)S(1)}, f32[32]{0:T(128)}, u32[]{:S(2)}) copy-start(f32[32]{0:T(128)} %param.20) | copy-start | bytes 388
  15.4 23.4 %copy-start.4 = (s32[512]{0:T(512)S(1)}, s32[512]{0:T(512)}, u32[]{:S(2)}) copy-start(s32[512]{0:T(512)} %param.22) | copy-start | bytes 6148
  15.4 23.4 %copy-start.5 = (s32[512]{0:T(512)S(1)}, s32[512]{0:T(512)}, u32[]{:S(2)}) copy-start(s32[512]{0:T(512)} %param.23) | copy-start | bytes 6148
  15.4 23.4 %copy-start.6 = (s32[512]{0:T(512)S(1)}, s32[512]{0:T(512)}, u32[]{:S(2)}) copy-start(s32[512]{0:T(512)} %param.21) | copy-start | bytes 6148
Sparse Core Ops, SparseCore 0:
  16.7 29.2 all-gather.3
where the time goes:
time: 157 us
  matrix products  59.4 us (38%)
  blocking collectives  59.1 us (38%)
  between operations  14.3 us (9%)
  local copies, waits for them, and re-layouts  12.3 us (8%)
  waiting for transfers between devices  6.65 us (4%)
  other arithmetic  4.69 us (3%)
    dot_general x8, matrix products, weigh_block(): jnp.einsum('tcj,tjp->tcp', fwd_table, spot, precision=HIGHEST_PREC)  50.4 us
    all_gather x2, blocking collectives, carried_in(): gathered = jax.tree.map(lambda a: lax.all_gather(a, axis), part)  25.5 us
    psum x1, blocking collectives, per_device(): profile = lax.psum(local_sum, 'path') / (total_paths * date_step)  15 us
    psum x1, blocking collectives, per_device(): lax.psum(LOSS_SHARE * date_step * jnp.sum(own_discount[:, None] * profile...  9.71 us
    unnamed x1, blocking collectives  8.93 us
    all_gather x1, waiting for transfers between devices, carried_in(): gathered = jax.tree.map(lambda a: lax.all_gather(a, axis), part)  6.64 us
    dot_general x1, matrix products, local_walk(): jnp.einsum('ts,jsp->tjp', lower_ones, moves, precision=HIGHEST_PREC)  5.52 us
    while x1, local copies, waits for them, and re-layouts, weigh_dates(): lax.map(lambda block_item: weigh_block(block_item, hazard_scale), blocks)  4.63 us
  transfers between devices with their start and end apart: 1, of which 1 were waited for; matrix products, arithmetic and copies ran while one was open for 2% of the time, Pallas kernels for 0%

commit v1 on v0

--- a/solution.py
+++ b/solution.py
@@ -10,6 +10,11 @@
 LOSS_SHARE = 0.6
 RATE_SHIFT = 1.5
 HIGHEST_PREC = lax.Precision.HIGHEST
+
+
+def summed_here(x, name):
+    shards = lax.all_gather(x, name)
+    return jnp.sum(shards, axis=0)
 
 
 def carried_in(part, axis, combine, identity):
@@ -171,7 +176,9 @@
     discount = jnp.exp(-RATE_DOM * date_step * (jnp.arange(total_dates, dtype=jnp.float32) + 1.0))
     profile = lax.psum(local_sum, "path") / (total_paths * date_step)
     own_discount = lax.dynamic_slice_in_dim(discount, first_date, local_dates, 0)
-    cva = lax.psum(LOSS_SHARE * date_step * jnp.sum(own_discount[:, None] * profile, axis=0), "tm")
+    cva = summed_here(
+        LOSS_SHARE * date_step * jnp.sum(own_discount[:, None] * profile, axis=0), "tm"
+    )
     return (profile, cva)
 
 

time: 157 us -> 157 us (level)
    psum x1 -> x0, blocking collectives: 9.71 us -> none  [per_device(): lax.psum(LOSS_SHARE * date_step * jnp.sum(own_discount[:, None] * profile...]
    unnamed x1 -> x2, blocking collectives: 8.93 us -> 18.2 us
    unnamed x23 -> x24, local copies, waits for them, and re-layouts: 3.53 us -> 3.51 us
where the time goes in v1:
time: 157 us
  matrix products  59.4 us (38%)
  blocking collectives  58.3 us (37%)
  between operations  14.9 us (9%)
  local copies, waits for them, and re-layouts  12.4 us (8%)
  waiting for transfers between devices  6.04 us (4%)
  other arithmetic  5.3 us (3%)
    dot_general x8, matrix products, weigh_block(): jnp.einsum('tcj,tjp->tcp', fwd_table, spot, precision=HIGHEST_PREC)  50.3 us
    all_gather x2, blocking collectives, carried_in(): gathered = jax.tree.map(lambda a: lax.all_gather(a, axis), part)  25.1 us
    unnamed x2, blocking collectives  18.2 us
    psum x1, blocking collectives, per_device(): profile = lax.psum(local_sum, 'path') / (total_paths * date_step)  15 us
    all_gather x1, waiting for transfers between devices, carried_in(): gathered = jax.tree.map(lambda a: lax.all_gather(a, axis), part)  6.03 us
    dot_general x1, matrix products, local_walk(): jnp.einsum('ts,jsp->tjp', lower_ones, moves, precision=HIGHEST_PREC)  5.52 us
    while x1, local copies, waits for them, and re-layouts, weigh_dates(): lax.map(lambda block_item: weigh_block(block_item, hazard_scale), blocks)  4.62 us
    unnamed x24, local copies, waits for them, and re-layouts  3.51 us
  transfers between devices with their start and end apart: 1, of which 1 were waited for; matrix products, arithmetic and copies ran while one was open for 2% of the time, Pallas kernels for 0%

profile of v1, /device:TPU:0, one launch (start us, length us, event | category | flops | bytes accessed | tf_op | source)
XLA Modules:
  0.0 156.8 jit_solution(5599662861464383986)
XLA Ops:
  7.9 5.5 %fusion.8 = f32[16,4,16384]{2,0,1:T(8,128)S(1)} fusion(f32[4,16,16384]{2,1,0:T(8,128)} %param.17, f32[4]{0:T(128)S(1)} %get-tuple-element.248, f32[4]{0:T(128)S(1)} %get-tuple-element.251, f32[16,16384]{1,0:T(8,128)} %param.16, f32[4]{0:T(128)} %param.19, f32[4]{0:T(128)S(1)} %get-tuple-element.247), kind=kOutput, calls=%fused_computation.23 | convolution fusion | flops 206569984 | bytes 9437248 | tf_op jit(solution)/shard_map/ts,jsp->tjp/dot_general | solution.py:96
  13.4 1.9 %copy-done = f32[16,4,16384]{2,0,1:T(8,128)} copy-done((f32[16,4,16384]{2,0,1:T(8,128)}, f32[16,4,16384]{2,0,1:T(8,128)S(1)}, u32[]{:S(2)}) %copy-start) | copy-done | bytes 4194328
  15.6 0.9 copy.15
  16.6 1.0 convolution_multiply_fusion.1
  17.6 10.5 %all-gather.2 = f32[4,1,16384]{2,1,0:T(1,128)S(1)} all-gather(f32[1,1,16384]{2,1,0:T(1,128)S(1)} %slice_bitcast_fusion), channel_id=1, replica_groups=mesh['path'=8,'tm'=4] {'tm'}, dimensions={0}, use_global_device_ids=true | all-gather | bytes 327680 | tf_op jit(solution)/shard_map/all_gather | solution.py:22
  28.7 0.7 dynamic-update-slice
  29.4 8.9 %all-reduce = f32[4]{0:T(128)S(1)} all-reduce(f32[4]{0:T(128)S(1)} %dynamic-update-slice), channel_id=1, replica_groups=mesh['path'=8,'tm'=4] {'tm'}, use_global_device_ids=true, to_apply=%add | all-reduce | flops 4 | bytes 32
  39.9 6.0 %all-gather.5.cloned.1.call-done = f32[4,4,16384]{2,1,0:T(4,128)} async-done(((f32[1,4,16384]{2,1,0:T(4,128)}), f32[4,4,16384]{2,1,0:T(4,128)}) %all-gather.5.cloned.1.call-update) | async-done | bytes 1048592 | tf_op jit(solution)/shard_map/all_gather | solution.py:22
  46.0 2.7 %add_exponential_fusion = f32[16,4,16384]{2,0,1:T(8,128)S(1)} fusion(f32[16,4,16384]{2,0,1:T(8,128)} %copy-done, f32[4,16384]{1,0:T(4,128)S(1)} %get-tuple-element.178), kind=kLoop, calls=%fused_computation.22 | loop fusion | flops 1048576 | bytes 8650752 | tf_op jit(solution)/shard_map/exp | solution.py:111
  48.7 4.6 %copy.18 = f32[16,4,16384]{2,1,0:T(4,128)} copy(f32[16,4,16384]{2,0,1:T(8,128)S(1)} %add_exponential_fusion) | data formatting | bytes 8388608 | tf_op jit(solution)/shard_map/while | solution.py:79
  53.8 14.7 %all-gather = f32[65536]{0:T(1024)S(1)} all-gather(f32[16384]{0:T(1024)S(1)} %broadcast_multiply_fusion), channel_id=2, replica_groups=mesh['path'=8,'tm'=4] {'tm'}, dimensions={0}, use_global_device_ids=true | all-gather | bytes 327680 | tf_op jit(solution)/shard_map/all_gather | solution.py:22
  68.8 2.1 %multiply_subtract_fusion = (f32[16,16384]{1,0:T(8,128)}, f32[16,16384]{1,0:T(8,128)S(1)}) fusion(f32[16,16384]{1,0:T(8,128)S(1)} %convolution_multiply_fusion.1, f32[16384]{0:T(1024)S(1)} %get-tuple-element.179, f32[16]{0:T(128)S(1)} %add_power_fusion, f32[16384]{0:T(1024)S(1)} %get-tuple-element.180), kind=kOutput, calls=%fused_computation.36 | convolution fusion | flops 54526464 | bytes 3276864 | tf_op jit(solution)/shard_map/dot_general | solution.py:107
  70.9 1.8 %reshape.78 = f32[8,2,16384]{2,1,0:T(2,128)S(1)} reshape(f32[16,16384]{1,0:T(8,128)} %get-tuple-element.249) | data formatting | bytes 2097152 | tf_op jit(solution)/shard_map/reshape | solution.py:76
  73.3 51.0 %while.38 = (s32[]{:T(128)}, f32[8,2,32]{2,1,0:T(2,128)S(1)}, f32[8,2,32,4]{2,1,0,3:T(2,128)S(1)}, f32[8,2,4,16384]{3,2,1,0:T(4,128)}, f32[8,2,32]{2,1,0:T(2,128...) while((s32[]{:T(128)}, f32[8,2,32]{2,1,0:T(2,128)S(1)}, ...), condition=%wide.region_7.8_spmd, body=%wide.region_5.7_spmd.sunk | while | flops 57671616 | bytes 1317113 | solution.py:79
  73.4 6.3 %fusion.73 = f32[2,32]{1,0:T(2,128)S(1)} fusion(f32[2,16384]{1,0:T(2,128)S(1)} %get-tuple-element.373, f32[2,16384]{1,0:T(2,128)S(1)} %get-tuple-element.374, f32[32]{0:T(128)S(1)} %bitcast.78, f32[2,32]{1,0:T(2,128)S(1)} %fusion.72, f32[8,2,4,16384]{3,2,1,0:T(4,128)} %get-tuple-element.447, s32[]{:T(128)S(6)} %copy.46, ...), kind=kOutput, calls=%fused_computation.8.clone.1 | convolution fusion | flops 57671616 | bytes 788100 | tf_op jit(solution)/shard_map/while/body/eval_jaxpr/tcj,tjp->tcp/dot_general | solution.py:56
  79.8 6.3 %fusion.73 = f32[2,32]{1,0:T(2,128)S(1)} fusion(f32[2,16384]{1,0:T(2,128)S(1)} %get-tuple-element.373, f32[2,16384]{1,0:T(2,128)S(1)} %get-tuple-element.374, f32[32]{0:T(128)S(1)} %bitcast.78, f32[2,32]{1,0:T(2,128)S(1)} %fusion.72, f32[8,2,4,16384]{3,2,1,0:T(4,128)} %get-tuple-element.447, s32[]{:T(128)S(6)} %copy.46, ...), kind=kOutput, calls=%fused_computation.8.clone.1 | convolution fusion | flops 57671616 | bytes 788100 | tf_op jit(solution)/shard_map/while/body/eval_jaxpr/tcj,tjp->tcp/dot_general | solution.py:56
  86.2 6.3 %fusion.73 = f32[2,32]{1,0:T(2,128)S(1)} fusion(f32[2,16384]{1,0:T(2,128)S(1)} %get-tuple-element.373, f32[2,16384]{1,0:T(2,128)S(1)} %get-tuple-element.374, f32[32]{0:T(128)S(1)} %bitcast.78, f32[2,32]{1,0:T(2,128)S(1)} %fusion.72, f32[8,2,4,16384]{3,2,1,0:T(4,128)} %get-tuple-element.447, s32[]{:T(128)S(6)} %copy.46, ...), kind=kOutput, calls=%fused_computation.8.clone.1 | convolution fusion | flops 57671616 | bytes 788100 | tf_op jit(solution)/shard_map/while/body/eval_jaxpr/tcj,tjp->tcp/dot_general | solution.py:56
  92.5 6.3 %fusion.73 = f32[2,32]{1,0:T(2,128)S(1)} fusion(f32[2,16384]{1,0:T(2,128)S(1)} %get-tuple-element.373, f32[2,16384]{1,0:T(2,128)S(1)} %get-tuple-element.374, f32[32]{0:T(128)S(1)} %bitcast.78, f32[2,32]{1,0:T(2,128)S(1)} %fusion.72, f32[8,2,4,16384]{3,2,1,0:T(4,128)} %get-tuple-element.447, s32[]{:T(128)S(6)} %copy.46, ...), kind=kOutput, calls=%fused_computation.8.clone.1 | convolution fusion | flops 57671616 | bytes 788100 | tf_op jit(solution)/shard_map/while/body/eval_jaxpr/tcj,tjp->tcp/dot_general | solution.py:56
  98.9 6.3 %fusion.73 = f32[2,32]{1,0:T(2,128)S(1)} fusion(f32[2,16384]{1,0:T(2,128)S(1)} %get-tuple-element.373, f32[2,16384]{1,0:T(2,128)S(1)} %get-tuple-element.374, f32[32]{0:T(128)S(1)} %bitcast.78, f32[2,32]{1,0:T(2,128)S(1)} %fusion.72, f32[8,2,4,16384]{3,2,1,0:T(4,128)} %get-tuple-element.447, s32[]{:T(128)S(6)} %copy.46, ...), kind=kOutput, calls=%fused_computation.8.clone.1 | convolution fusion | flops 57671616 | bytes 788100 | tf_op jit(solution)/shard_map/while/body/eval_jaxpr/tcj,tjp->tcp/dot_general | solution.py:56
  105.3 6.3 %fusion.73 = f32[2,32]{1,0:T(2,128)S(1)} fusion(f32[2,16384]{1,0:T(2,128)S(1)} %get-tuple-element.373, f32[2,16384]{1,0:T(2,128)S(1)} %get-tuple-element.374, f32[32]{0:T(128)S(1)} %bitcast.78, f32[2,32]{1,0:T(2,128)S(1)} %fusion.72, f32[8,2,4,16384]{3,2,1,0:T(4,128)} %get-tuple-element.447, s32[]{:T(128)S(6)} %copy.46, ...), kind=kOutput, calls=%fused_computation.8.clone.1 | convolution fusion | flops 57671616 | bytes 788100 | tf_op jit(solution)/shard_map/while/body/eval_jaxpr/tcj,tjp->tcp/dot_general | solution.py:56
  111.6 6.3 %fusion.73 = f32[2,32]{1,0:T(2,128)S(1)} fusion(f32[2,16384]{1,0:T(2,128)S(1)} %get-tuple-element.373, f32[2,16384]{1,0:T(2,128)S(1)} %get-tuple-element.374, f32[32]{0:T(128)S(1)} %bitcast.78, f32[2,32]{1,0:T(2,128)S(1)} %fusion.72, f32[8,2,4,16384]{3,2,1,0:T(4,128)} %get-tuple-element.447, s32[]{:T(128)S(6)} %copy.46, ...), kind=kOutput, calls=%fused_computation.8.clone.1 | convolution fusion | flops 57671616 | bytes 788100 | tf_op jit(solution)/shard_map/while/body/eval_jaxpr/tcj,tjp->tcp/dot_general | solution.py:56
  118.0 6.3 %fusion.73 = f32[2,32]{1,0:T(2,128)S(1)} fusion(f32[2,16384]{1,0:T(2,128)S(1)} %get-tuple-element.373, f32[2,16384]{1,0:T(2,128)S(1)} %get-tuple-element.374, f32[32]{0:T(128)S(1)} %bitcast.78, f32[2,32]{1,0:T(2,128)S(1)} %fusion.72, f32[8,2,4,16384]{3,2,1,0:T(4,128)} %get-tuple-element.447, s32[]{:T(128)S(6)} %copy.46, ...), kind=kOutput, calls=%fused_computation.8.clone.1 | convolution fusion | flops 57671616 | bytes 788100 | tf_op jit(solution)/shard_map/while/body/eval_jaxpr/tcj,tjp->tcp/dot_general | solution.py:56
  124.3 15.0 %psum.7 = f32[16,32]{1,0:T(8,128)S(1)} all-reduce(f32[16,32]{1,0:T(8,128)S(1)} %bitcast.75), channel_id=1, replica_groups=mesh['path'=8,'tm'=4] {'path'}, use_global_device_ids=true, to_apply=%region_8.9 | all-reduce | flops 512 | bytes 4096 | tf_op jit(solution)/shard_map/psum | solution.py:177
  140.1 9.2 %all-reduce.1 = f32[128]{0:T(128)S(1)} all-reduce(f32[128]{0:T(128)S(1)} %multiply_dynamic-update-slice_fusion), channel_id=3, replica_groups=mesh['path'=8,'tm'=4] {'tm'}, use_global_device_ids=true, to_apply=%add.1 | all-reduce | flops 128 | bytes 1024
  (82 shorter events, 5.6 us)
Async XLA Ops:
  7.2 38.7 %all-gather.5.cloned.1.call-start = ((), (), s32[]{:S(2)}) async-start(), calls=%async_computation | async-start | bytes 1310720 | tf_op jit(solution)/shard_map/all_gather | solution.py:22
  7.9 8.7 %copy-start.1 = (f32[16,16384]{1,0:T(8,128)S(1)}, f32[16,16384]{1,0:T(8,128)}, u32[]{:S(2)}) copy-start(f32[16,16384]{1,0:T(8,128)} %param.16) | copy-start | bytes 3145732
  7.9 20.2 %copy-start.8 = (u32[32]{0:T(128)S(1)}, u32[32]{0:T(128)}, u32[]{:S(2)}) copy-start(u32[32]{0:T(128)} %constant.112) | copy-start | bytes 388
  13.4 1.9 %copy-start = (f32[16,4,16384]{2,0,1:T(8,128)}, f32[16,4,16384]{2,0,1:T(8,128)S(1)}, u32[]{:S(2)}) copy-start(f32[16,4,16384]{2,0,1:T(8,128)S(1)} %fusion.8) | copy-start | bytes 12582916
  15.3 23.8 %copy-start.2 = (f32[512]{0:T(512)S(1)}, f32[512]{0:T(512)}, u32[]{:S(2)}) copy-start(f32[512]{0:T(512)} %param.24) | copy-start | bytes 6148
  15.4 23.8 %copy-start.3 = (f32[512]{0:T(512)S(1)}, f32[512]{0:T(512)}, u32[]{:S(2)}) copy-start(f32[512]{0:T(512)} %param.25) | copy-start | bytes 6148
  15.4 24.0 %copy-start.7 = (f32[32]{0:T(128)S(1)}, f32[32]{0:T(128)}, u32[]{:S(2)}) copy-start(f32[32]{0:T(128)} %param.20) | copy-start | bytes 388
  15.4 24.0 %copy-start.4 = (s32[512]{0:T(512)S(1)}, s32[512]{0:T(512)}, u32[]{:S(2)}) copy-start(s32[512]{0:T(512)} %param.22) | copy-start | bytes 6148
  15.4 24.0 %copy-start.5 = (s32[512]{0:T(512)S(1)}, s32[512]{0:T(512)}, u32[]{:S(2)}) copy-start(s32[512]{0:T(512)} %param.23) | copy-start | bytes 6148
  15.4 24.0 %copy-start.6 = (s32[512]{0:T(512)S(1)}, s32[512]{0:T(512)}, u32[]{:S(2)}) copy-start(s32[512]{0:T(512)} %param.21) | copy-start | bytes 6148
Sparse Core Ops, SparseCore 0:
  16.6 29.2 all-gather.4
